TPU v7x, 32 devices: a whole 2x2x4 slice. The times are simulated.
32 devices in a mesh: member: 2 (over x), lat: 16 (over z, y, core).
Axes of the slice: x: 2, y: 2, z: 4, core: 2. Of those that a mesh axis runs over, the one named last changes fastest.
Arguments:
- field: bfloat16 [192, 1440, 256], P(('member', 'lat')), parts along dimension 0, may hold values from -3000 to 3000
- gain: float32 [256], replicated, may hold values from 0.1 to 1.9
- slot_wave: int32 [96], replicated, may hold values from 0 to 96, as said below
- legendre: bfloat16 [96, 96, 96], P('lat'), may hold values from -0.625 to 0.625
- mixing: bfloat16 [96, 2, 256, 256], P('lat'), may hold values from -0.25 to 0.25
Outputs:
- result: bfloat16 [192, 1440, 256], P(('member', 'lat')), parts along dimension 0
There are 2 independent parts, one for each index of `member`. A program takes and returns all parts, laid end to end along the dimension named above; an argument that names none is the same for every part. Nothing has to cross between parts.
Inputs may be any that keep to these rules, and one draw needn't show every extreme that they name: `slot_wave`: each wavenumber 0 to 95 stands in exactly one slot and every other slot holds 96; slots 2k and 2k+1 of one lat index hold wavenumbers adding up to (4k+2)16 - 1 where both are below 96.
All inputs are finite; a program needn't handle non-finite values.
Results may differ from a plain program's by a relative error of at most 0.0085.
Values may be sent and summed in bfloat16 or wider, within the bound.
No kernel may reach another device: no remote copies, remote signals or barrier semaphores. Data moves between devices by JAX's collectives and lax.ppermute only.
A program may use at most 64 MiB of HBM per device.

v0:
```python
import math

import jax
import jax.numpy as jnp
from jax import lax
from jax.sharding import PartitionSpec as P


def phase_tables(waves, width):
    points = jnp.arange(width, dtype=jnp.int32)
    phase = (waves[:, None] * points[None, :] % width).astype(jnp.float32) * (2.0 * math.pi / width)
    return (jnp.cos(phase), jnp.sin(phase))


def block_weight(mixing):
    real_part = mixing[:, 0]
    imag_part = mixing[:, 1]
    upper = jnp.concatenate([real_part, imag_part], axis=2)
    lower = jnp.concatenate([-imag_part, real_part], axis=2)
    return jnp.concatenate([upper, lower], axis=1)


def per_device(field, gain, slot_wave, legendre, mixing):
    lat_count = lax.axis_size("lat")
    lat_dev, width, chans = field.shape
    slot_dev, degs, nlat = legendre.shape
    count = float(lat_dev * lat_count * width)
    values = field.astype(jnp.float32)
    local_sum = jnp.sum(values, axis=(0, 1))
    local_sq = jnp.sum(values * values, axis=(0, 1))
    total, squares = lax.psum((local_sum, local_sq), "lat")
    mean = total / count
    var = squares / count - mean * mean
    normed = ((values - mean) * (gain / jnp.sqrt(var + 1e-05))).astype(jnp.bfloat16)
    cosine, sine = phase_tables(slot_wave, width)
    forward = jnp.stack([cosine, -sine]).astype(jnp.bfloat16).reshape(2, lat_count, slot_dev, width)
    weight_m = jnp.where(slot_wave == 0, 1.0, 2.0).astype(jnp.float32)[:, None]
    inverse = jnp.stack([weight_m * cosine, -weight_m * sine]).astype(jnp.bfloat16)
    inv_root = 1.0 / math.sqrt(width)
    spectrum = (
        jnp.einsum("anc,rdjn->dajrc", normed, forward, preferred_element_type=jnp.float32)
        * inv_root
    )
    spectrum = spectrum.astype(jnp.bfloat16).reshape(lat_count, lat_dev, slot_dev, 2 * chans)
    arrived = lax.all_to_all(spectrum, "lat", split_axis=0, concat_axis=1, tiled=True)[0]
    mine = lax.dynamic_slice_in_dim(slot_wave, lax.axis_index("lat") * slot_dev, slot_dev, 0)
    big = block_weight(mixing)
    lat_scale = math.sqrt(nlat / degs)
    degrees = jnp.arange(degs, dtype=jnp.int32)
    coef = jnp.einsum("jlt,tjc->jlc", legendre, arrived, preferred_element_type=jnp.float32)
    coef = jnp.where((degrees[None, :] >= mine[:, None])[:, :, None], coef, 0.0).astype(
        jnp.bfloat16
    )
    mixed = jnp.einsum("jlc,jcd->jld", coef, big, preferred_element_type=jnp.float32).astype(
        jnp.bfloat16
    )
    back = (
        jnp.einsum("jlt,jld->tjd", legendre, mixed, preferred_element_type=jnp.float32) * lat_scale
    )
    back = back.astype(jnp.bfloat16)
    back = back.reshape(lat_count, lat_dev, slot_dev, 2 * chans)
    returned = lax.all_to_all(back, "lat", split_axis=0, concat_axis=2, tiled=True)[0]
    returned = returned.reshape(lat_dev, slot_dev * lat_count, 2, chans)
    filtered = (
        jnp.einsum("akrc,rkn->anc", returned, inverse, preferred_element_type=jnp.float32)
        * inv_root
    )
    return (normed.astype(jnp.float32) + filtered).astype(jnp.bfloat16)


def solution(mesh):
    return jax.shard_map(
        per_device,
        mesh=mesh,
        in_specs=(
            P(("member", "lat"), None, None),
            P(),
            P(),
            P("lat", None, None),
            P("lat", None, None, None),
        ),
        out_specs=P(("member", "lat"), None, None),
        check_vma=False,
    )
```

profile of v0, /device:TPU:0, one launch (start us, length us, event | category | flops | bytes accessed | tf_op | source)
XLA Modules:
  0.0 103.8 jit_solution(11740767256744801090)
XLA Ops:
  0.0 0.0 copy-start
  0.0 0.0 copy-start.2
  0.0 0.0 copy-start.3
  0.0 3.5 %convert_reduce_fusion = (f32[256]{0:T(256)S(1)}, f32[256]{0:T(256)S(1)}) fusion(bf16[6,1440,256]{2,1,0:T(8,128)(2,1)} %param.5), kind=kLoop, calls=%fused_computation.2 | loop fusion | flops 8846848 | bytes 4425728 | tf_op jit(solution)/shard_map/reduce_sum | solution.py:29
  3.5 0.0 copy-done.2
  3.5 0.1 mul.154
  3.6 0.1 copy.23
  3.7 2.8 %cosine_convert_fusion = (bf16[1,16,6,1440]{3,1,2,0:T(8,128)(2,1)S(1)}, bf16[1,16,6,1440]{3,1,2,0:T(8,128)(2,1)S(1)}) fusion(s32[16,6]{0,1:T(8,128)S(1)} %copy.23), kind=kLoop, calls=%fused_computation.44 | loop fusion | flops 1658880 | bytes 553344 | tf_op jit(solution)/shard_map/convert
  6.5 35.0 %all-reduce = (f32[256]{0:T(256)S(1)}, f32[256]{0:T(256)S(1)}) all-reduce(f32[256]{0:T(256)S(1)} %get-tuple-element.6, f32[256]{0:T(256)S(1)} %get-tuple-element.5), channel_id=1, replica_groups=mesh['member'=2,'lat'=16] {'lat'}, use_global_device_ids=true, to_apply=%region_3.0 | all-reduce | flops 512 | bytes 4096 | tf_op jit(solution)/shard_map/psum | solution.py:31
  41.5 0.0 copy-done.3
  41.5 3.6 %fusion.26 = bf16[16,6,6,2,256]{4,0,1,2,3:T(8,128)(2,1)S(1)} fusion(f32[256]{0:T(256)S(1)} %get-tuple-element.14, f32[256]{0:T(256)S(1)} %get-tuple-element.13, bf16[6,1440,256]{2,1,0:T(8,128)(2,1)} %param.5, bf16[1,16,6,1440]{3,1,2,0:T(8,128)(2,1)S(1)} %get-tuple-element.12, bf16[1,16,6,1440]{3,1,2,0:T(8,128)(2,1)S(1)} %get-tuple-element.11), kind=kOutput, calls=%fused_computation.26 | convolution fusion | flops 859889664 | bytes 5568512 | tf_op jit(solution)/shard_map/anc,rdjn->dajrc/dot_general | solution.py:41
  45.1 0.0 copy-start.1
  45.1 0.6 copy.37
  45.8 1.3 %reshape.223 = bf16[16,6,6,512]{3,2,1,0:T(8,128)(2,1)} reshape(bf16[16,6,6,2,256]{4,3,2,1,0:T(2,128)(2,1)S(1)} %copy.37) | data formatting | bytes 1179648 | tf_op jit(solution)/shard_map/reshape | solution.py:44
  47.0 3.6 %all-to-all-start = ((bf16[16,6,6,512]{3,2,1,0:T(8,128)(2,1)}), bf16[16,6,6,512]{3,2,1,0:T(8,128)(2,1)S(1)}, u32[]{:S(2)}, u32[]{:S(2)}) async-start(bf16[16,6,6,512]{3,2,1,0:T(8,128)(2,1)} %reshape.223), calls=%async_computation | async-start | bytes 1572864 | tf_op jit(solution)/shard_map/all_to_all | solution.py:45
  50.7 0.1 dynamic_slice.3
  50.7 0.1 iota_compare_fusion
  50.8 0.0 copy-done.1
  50.8 0.1 fusion.52
  50.9 1.3 %slice_bitcast_fusion = (bf16[6,256,256]{2,1,0:T(8,128)(2,1)}, bf16[6,256,256]{2,1,0:T(8,128)(2,1)}) fusion(bf16[6,2,256,256]{3,2,1,0:T(8,128)(2,1)S(1)} %copy-done.1), kind=kLoop, calls=%fused_computation.29 | loop fusion | bytes 3145728 | tf_op jit(solution)/shard_map/squeeze | solution.py:17
  52.1 17.2 %all-to-all-done = bf16[16,6,6,512]{3,2,1,0:T(8,128)(2,1)S(1)} async-done(((bf16[16,6,6,512]{3,2,1,0:T(8,128)(2,1)}), bf16[16,6,6,512]{3,2,1,0:T(8,128)(2,1)S(1)}, u32[]{:S(2)}, u32[]{:S(2)}) %all-to-all-start) | async-done | bytes 589856 | tf_op jit(solution)/shard_map/all_to_all | solution.py:45
  69.3 0.0 copy-done
  69.3 0.4 fusion.18
  69.7 2.4 %fusion.25 = bf16[96,6,512]{2,0,1:T(8,128)(2,1)S(1)} fusion(bf16[6,96,96]{2,1,0:T(8,128)(2,1)S(1)} %copy-done, bf16[6,512,96]{1,2,0:T(8,128)(2,1)S(1)} %fusion.18, bf16[6,256,256]{2,1,0:T(8,128)(2,1)} %get-tuple-element.10, bf16[6,256,256]{2,1,0:T(8,128)(2,1)S(1)} %fusion.52, bf16[6,256,256]{2,1,0:T(8,128)(2,1)} %get-tuple-element.9), kind=kOutput, calls=%fused_computation.25 | convolution fusion | flops 371785728 | bytes 3649536 | tf_op jit(solution)/shard_map/jlt,jld->tjd/dot_general | solution.py:58
  72.1 0.2 reshape.218
  72.3 1.0 copy.30
  73.3 5.3 %all-to-all-start.1 = ((bf16[16,6,6,512]{3,1,2,0:T(8,128)(2,1)}), bf16[16,6,6,512]{3,1,2,0:T(8,128)(2,1)S(1)}, u32[]{:S(2)}, u32[]{:S(2)}) async-start(bf16[16,6,6,512]{3,1,2,0:T(8,128)(2,1)} %copy.30), calls=%async_computation.1 | async-start | bytes 1572864 | tf_op jit(solution)/shard_map/all_to_all | solution.py:62
  78.6 2.9 %multiply_convert_fusion.1 = (bf16[1,96,1440]{2,1,0:T(8,128)(2,1)S(1)}, bf16[1,96,1440]{2,1,0:T(8,128)(2,1)S(1)}) fusion(s32[96]{0:T(128)S(1)} %copy-done.2, f32[96]{0:T(128)S(1)} %get-tuple-element.17, f32[96]{0:T(128)S(1)} %get-tuple-element.18), kind=kLoop, calls=%fused_computation.49 | loop fusion | flops 1797120 | bytes 554112 | tf_op jit(solution)/shard_map/convert.2
  81.5 15.8 %all-to-all-done.1 = bf16[16,6,6,512]{3,1,2,0:T(8,128)(2,1)S(1)} async-done(((bf16[16,6,6,512]{3,1,2,0:T(8,128)(2,1)}), bf16[16,6,6,512]{3,1,2,0:T(8,128)(2,1)S(1)}, u32[]{:S(2)}, u32[]{:S(2)}) %all-to-all-start.1) | async-done | bytes 589856 | tf_op jit(solution)/shard_map/all_to_all | solution.py:62
  97.3 0.3 reshape.224
  97.6 6.2 %fusion.3 = bf16[6,1440,256]{2,1,0:T(8,128)(2,1)} fusion(f32[256]{0:T(256)S(1)} %get-tuple-element.14, f32[256]{0:T(256)S(1)} %get-tuple-element.13, bf16[6,1440,256]{2,1,0:T(8,128)(2,1)} %param.5, bf16[1,96,1440]{2,1,0:T(8,128)(2,1)S(1)} %get-tuple-element.16, bf16[1,96,1440]{2,1,0:T(8,128)(2,1)S(1)} %get-tuple-element.15, ...), kind=kOutput, calls=%fused_computation.7 | convolution fusion | flops 868147200 | bytes 9992192 | tf_op jit(solution)/shard_map/akrc,rkn->anc/dot_general | solution.py:65
  (2 shorter events, 0.0 us)
Async XLA Ops:
  0.0 69.3 %copy-start = (bf16[6,96,96]{2,1,0:T(8,128)(2,1)S(1)}, bf16[6,96,96]{2,1,0:T(8,128)(2,1)}, u32[]{:S(2)}) copy-start(bf16[6,96,96]{2,1,0:T(8,128)(2,1)} %param.8) | copy-start | bytes 331780
  0.0 3.5 %copy-start.2 = (s32[96]{0:T(128)S(1)}, s32[96]{0:T(128)}, u32[]{:S(2)}) copy-start(s32[96]{0:T(128)} %param.7) | copy-start | bytes 1156
  0.0 41.5 %copy-start.3 = (f32[256]{0:T(256)S(1)}, f32[256]{0:T(256)}, u32[]{:S(2)}) copy-start(f32[256]{0:T(256)} %param.6) | copy-start | bytes 3076
  45.1 5.7 %copy-start.1 = (bf16[6,2,256,256]{3,2,1,0:T(8,128)(2,1)S(1)}, bf16[6,2,256,256]{3,2,1,0:T(8,128)(2,1)}, u32[]{:S(2)}) copy-start(bf16[6,2,256,256]{3,2,1,0:T(8,128)(2,1)} %param.9) | copy-start | bytes 4718596
  47.0 22.3 %all-to-all-start = ((bf16[16,6,6,512]{3,2,1,0:T(8,128)(2,1)}), bf16[16,6,6,512]{3,2,1,0:T(8,128)(2,1)S(1)}, u32[]{:S(2)}, u32[]{:S(2)}) async-start(bf16[16,6,6,512]{3,2,1,0:T(8,128)(2,1)} %reshape.223), calls=%async_computation | async-start | bytes 1572864 | tf_op jit(solution)/shard_map/all_to_all | solution.py:45
  73.3 24.0 %all-to-all-start.1 = ((bf16[16,6,6,512]{3,1,2,0:T(8,128)(2,1)}), bf16[16,6,6,512]{3,1,2,0:T(8,128)(2,1)S(1)}, u32[]{:S(2)}, u32[]{:S(2)}) async-start(bf16[16,6,6,512]{3,1,2,0:T(8,128)(2,1)} %copy.30), calls=%async_computation.1 | async-start | bytes 1572864 | tf_op jit(solution)/shard_map/all_to_all | solution.py:62
where the time goes:
time: 104 us
  blocking collectives  35 us (34%)
  waiting for transfers between devices  33 us (32%)
  matrix products  12.6 us (12%)
  other arithmetic  9.31 us (9%)
  starting transfers between devices  8.95 us (9%)
  local copies, waits for them, and re-layouts  4.87 us (5%)
    psum x1, blocking collectives, per_device(): total, squares = lax.psum((local_sum, local_sq), 'lat')  35 us
    all_to_all x1, waiting for transfers between devices, per_device(): lax.all_to_all(spectrum, 'lat', split_axis=0, concat_axis=1, tiled=True)[0]  17.2 us
    all_to_all x1, waiting for transfers between devices, per_device(): lax.all_to_all(back, 'lat', split_axis=0, concat_axis=2, tiled=True)[0]  15.8 us
    dot_general x1, matrix products, per_device(): jnp.einsum('akrc,rkn->anc', returned, inverse, preferred_element_type=jnp...  6.16 us
    another operation x2, other arithmetic  5.69 us
    all_to_all x1, starting transfers between devices, per_device(): lax.all_to_all(back, 'lat', split_axis=0, concat_axis=2, tiled=True)[0]  5.33 us
    dot_general x1, matrix products, per_device(): jnp.einsum('anc,rdjn->dajrc', normed, forward, preferred_element_type=jnp...  3.65 us
    all_to_all x1, starting transfers between devices, per_device(): lax.all_to_all(spectrum, 'lat', split_axis=0, concat_axis=1, tiled=True)[0]  3.61 us
  transfers between devices with their start and end apart: 2, of which 2 were waited for; matrix products, arithmetic and copies ran while one was open for 4% of the time, Pallas kernels for 0%

commit v1 on v0

v1 whole, which is shorter than its diff:
```python
import functools
import math

import jax
import jax.numpy as jnp
import numpy as np
from jax import lax
from jax.experimental import pallas as pl
from jax.experimental.pallas import tpu as pltpu
from jax.sharding import PartitionSpec as P

F32 = jnp.float32
BF16 = jnp.bfloat16
PIECES = 3
EXTRA = 16


def dot(a, b, dims=((1,), (0,))):
    return lax.dot_general(a, b, (dims, ((), ())), preferred_element_type=F32)


def wave_tables(degs, width):
    turns = np.outer(np.arange(degs), np.arange(width)) % width
    phase = turns.astype(np.float64) * (2.0 * math.pi / width)
    table = np.concatenate([np.cos(phase), -np.sin(phase)]).astype(BF16)
    return table, table.astype(np.float64).sum(axis=1).astype(np.float32)


def forward_kernel(field, table, sums, column, payload, spec, packed, first, acc):
    step = pl.program_id(0)
    steps, rows, chans = spec.shape
    degs = rows // 2
    width = field.shape[1]
    block = field[0]

    @pl.when(step == 0)
    def _():
        first[...] = jnp.broadcast_to(block[0:1].astype(F32), first.shape)
        acc[...] = jnp.zeros_like(acc)

    spec[step] = dot(table[...], block)
    shifted = block.astype(F32).reshape(width // 8, 8, chans) - first[...]
    acc[0] += jnp.sum(shifted, axis=0)
    acc[1] += jnp.sum(shifted * shifted, axis=0)

    @pl.when(step == steps - 1)
    def _():
        count = float(steps * width)
        shift = jnp.sum(acc[0], axis=0, keepdims=True) / count
        square = jnp.sum(acc[1], axis=0, keepdims=True)
        mean = first[0:1] + shift
        spread = jnp.maximum(square - count * shift * shift, 0.0)
        for a in range(steps):
            centred = (spec[a] - sums[...] * mean).astype(BF16)
            packed[a * degs : (a + 1) * degs, :chans] = centred[:degs]
            packed[a * degs : (a + 1) * degs, chans:] = centred[degs:]
        rest = jnp.concatenate([mean, spread], axis=1)
        lane = lax.broadcasted_iota(jnp.int32, (EXTRA, 2 * chans), 0)
        tail = jnp.zeros((EXTRA, 2 * chans), F32)
        for piece in range(PIECES):
            part = rest.astype(BF16).astype(F32)
            tail = jnp.where(lane == piece, part, tail)
            rest = rest - part
        packed[steps * degs :, :] = tail.astype(BF16)
        total = payload.shape[0]
        chunk = total // 2 if total <= 1024 else total // 8
        for start in range(0, total, chunk):
            pick = lax.broadcasted_iota(jnp.int32, (chunk, packed.shape[0]), 1)
            pick = (pick == column[start : start + chunk]).astype(F32).astype(BF16)
            payload[start : start + chunk] = dot(pick, packed[...]).astype(BF16)


def spread_kernel(legendre, place, out):
    slots, degs, nlat = legendre.shape
    total = out.shape[1]
    lat = lax.broadcasted_iota(jnp.int32, (nlat, total), 0)
    for j in range(slots):
        pick = (lat == place[j : j + 1]).astype(F32).astype(BF16)
        out[j * degs : (j + 1) * degs] = dot(legendre[j], pick).astype(BF16)


def spectral_kernel(
    lat_count, count, inv_root, lat_scale, mine, arrived, wide, mixing, gain, sums, back, norm, mixed
):
    total, lanes = arrived.shape
    chans = lanes // 2
    rows = total // lat_count
    slots = mixing.shape[0]
    degs = wide.shape[0] // slots
    data = arrived[...]
    pick_row = lax.broadcasted_iota(jnp.int32, (PIECES * lat_count, total), 0)
    pick_col = lax.broadcasted_iota(jnp.int32, (PIECES * lat_count, total), 1)
    base = rows - 4
    want = (pick_row % lat_count) * rows + base + pick_row // lat_count
    stats = dot((pick_col == want).astype(F32).astype(BF16), data)
    stats = stats.reshape(PIECES, lat_count, lanes)
    stats = stats[0] + (stats[1] + stats[2])
    means = stats[:, :chans]
    mean = jnp.sum(means, axis=0, keepdims=True) / lat_count
    offs = means - mean
    var = jnp.sum(stats[:, chans:] + count * offs * offs, axis=0, keepdims=True) / (
        count * lat_count
    )
    scale = gain[...] / jnp.sqrt(var + 1e-05)
    norm[0:1] = mean
    norm[1:2] = scale
    scale2 = jnp.concatenate([scale, scale], axis=1) * inv_root
    offs2 = jnp.concatenate([offs, offs], axis=1)
    full = data.astype(F32).reshape(lat_count, rows, lanes)
    full = (full + offs2[:, None, :] * sums[...][None]) * scale2[None]
    full = full.reshape(total, lanes).astype(BF16)
    degree = lax.broadcasted_iota(jnp.int32, (degs, lanes), 0)
    for j in range(slots):
        wave = mine[j]
        coef = dot(wide[j * degs : (j + 1) * degs], full)
        coef = jnp.where(degree >= wave, coef, 0.0).astype(BF16)
        re, im = coef[:, :chans], coef[:, chans:]
        w0, w1 = mixing[j, 0], mixing[j, 1]
        weight = jnp.where(wave == 0, 1.0, 2.0).astype(F32)
        out_re = (dot(re, w0) - dot(im, w1)).astype(BF16).astype(F32) * weight
        out_im = (dot(re, w1) + dot(im, w0)).astype(BF16).astype(F32) * weight
        mixed[j * degs : (j + 1) * degs, :chans] = out_re.astype(BF16)
        mixed[j * degs : (j + 1) * degs, chans:] = out_im.astype(BF16)
    back[...] = (dot(wide[...], mixed[...], ((0,), (0,))) * lat_scale).astype(BF16)


def inverse_kernel(inv_root, field, returned, column, table, norm, result, waves):
    lats, rows, chans = waves.shape
    degs = rows // 2
    total = returned.shape[0]

    @pl.when((pl.program_id(0) == 0) & (pl.program_id(1) == 0))
    def _():
        for a in range(lats):
            pick = lax.broadcasted_iota(jnp.int32, (degs, total), 0) + a * degs
            pick = (pick == column[...]).astype(F32).astype(BF16)
            value = dot(pick, returned[...]).astype(BF16)
            waves[a, :degs] = value[:, :chans]
            waves[a, degs:] = value[:, chans:]

    filtered = dot(table[...], waves[pl.program_id(0)]) * inv_root
    normed = ((field[0].astype(F32) - norm[0:1]) * norm[1:2]).astype(BF16).astype(F32)
    result[0] = (normed + filtered).astype(BF16)


def per_device(field, gain, slot_wave, legendre, mixing):
    lat_count = lax.axis_size("lat")
    lat_dev, width, chans = field.shape
    slot_dev, degs, nlat = legendre.shape
    lanes = 2 * chans
    data_rows = lat_dev * slot_dev
    rows = -(-(data_rows + PIECES + 1) // 8) * 8
    total = lat_count * rows
    inv_root = 1.0 / math.sqrt(width)
    table, sums = wave_tables(degs, width)
    whole = pl.BlockSpec(memory_space=pltpu.VMEM)

    waves = slot_wave.reshape(lat_count, slot_dev, 1)
    source = jnp.arange(lat_dev, dtype=jnp.int32)[None, None, :] * degs + waves
    source = jnp.where(waves < degs, source, -1).reshape(lat_count, data_rows)
    tail = np.full((lat_count, rows - data_rows), -1, np.int32)
    tail[:, rows - data_rows - 4 : rows - data_rows - 4 + PIECES] = lat_dev * degs + np.arange(PIECES)
    column = jnp.concatenate([source, jnp.asarray(tail)], axis=1)

    steps = lat_dev
    payload = pl.pallas_call(
        forward_kernel,
        grid=(steps,),
        in_specs=[
            pl.BlockSpec((1, width, chans), lambda i: (i, 0, 0)),
            pl.BlockSpec((2 * degs, width), lambda i: (0, 0)),
            pl.BlockSpec((2 * degs, 1), lambda i: (0, 0)),
            pl.BlockSpec((total, 1), lambda i: (0, 0)),
        ],
        out_specs=pl.BlockSpec((total, lanes), lambda i: (0, 0)),
        out_shape=jax.ShapeDtypeStruct((total, lanes), BF16),
        scratch_shapes=[
            pltpu.VMEM((steps, 2 * degs, chans), F32),
            pltpu.VMEM((steps * degs + EXTRA, lanes), BF16),
            pltpu.VMEM((8, chans), F32),
            pltpu.VMEM((2, 8, chans), F32),
        ],
        compiler_params=pltpu.CompilerParams(dimension_semantics=("arbitrary",)),
        name="forward",
    )(field, jnp.asarray(table), jnp.asarray(sums)[:, None], column.reshape(total, 1))
    arrived = lax.all_to_all(
        payload.reshape(lat_count, rows, lanes), "lat", split_axis=0, concat_axis=0, tiled=True
    ).reshape(total, lanes)

    place = np.full((slot_dev, lat_count, rows), -1, np.int32)
    for j in range(slot_dev):
        place[j, :, j * lat_dev : (j + 1) * lat_dev] = np.arange(nlat).reshape(lat_count, lat_dev)
    wide = pl.pallas_call(
        spread_kernel,
        in_specs=[whole, whole],
        out_specs=whole,
        out_shape=jax.ShapeDtypeStruct((slot_dev * degs, total), BF16),
        cost_estimate=pl.CostEstimate(
            flops=2 * slot_dev * degs * nlat * total, bytes_accessed=0, transcendentals=0
        ),
        name="spread",
    )(legendre, jnp.asarray(place.reshape(slot_dev, total)))

    mine = lax.dynamic_slice_in_dim(slot_wave, lax.axis_index("lat") * slot_dev, slot_dev, 0)
    pair = jnp.asarray(np.stack([sums[:degs], sums[degs:]]))
    known = jnp.where(mine < degs, pair[:, jnp.minimum(mine, degs - 1)], 0.0)
    known = jnp.repeat(known, lat_dev, axis=1)
    known = jnp.pad(known, ((0, 0), (0, rows - data_rows)))
    known = jnp.broadcast_to(known.T[:, :, None], (rows, 2, chans)).reshape(rows, lanes)
    back, norm = pl.pallas_call(
        functools.partial(
            spectral_kernel,
            lat_count,
            float(lat_dev * width),
            inv_root,
            math.sqrt(nlat / degs),
        ),
        in_specs=[pl.BlockSpec(memory_space=pltpu.SMEM)] + [whole] * 5,
        out_specs=(whole, whole),
        out_shape=(
            jax.ShapeDtypeStruct((total, lanes), BF16),
            jax.ShapeDtypeStruct((8, chans), F32),
        ),
        scratch_shapes=[pltpu.VMEM((slot_dev * degs, lanes), BF16)],
        name="spectral",
    )(mine, arrived, wide, mixing, gain[None], known)
    returned = lax.all_to_all(
        back.reshape(lat_count, rows, lanes), "lat", split_axis=0, concat_axis=0, tiled=True
    ).reshape(total, lanes)

    parts = 2
    return pl.pallas_call(
        functools.partial(inverse_kernel, inv_root),
        grid=(lat_dev, parts),
        in_specs=[
            pl.BlockSpec((1, width // parts, chans), lambda i, k: (i, k, 0)),
            pl.BlockSpec((total, lanes), lambda i, k: (0, 0)),
            pl.BlockSpec((1, total), lambda i, k: (0, 0)),
            pl.BlockSpec((width // parts, 2 * degs), lambda i, k: (k, 0)),
            pl.BlockSpec((8, chans), lambda i, k: (0, 0)),
        ],
        out_specs=pl.BlockSpec((1, width // parts, chans), lambda i, k: (i, k, 0)),
        out_shape=jax.ShapeDtypeStruct(field.shape, BF16),
        scratch_shapes=[pltpu.VMEM((lat_dev, 2 * degs, chans), BF16)],
        compiler_params=pltpu.CompilerParams(dimension_semantics=("arbitrary", "arbitrary")),
        name="inverse",
    )(field, returned, column.reshape(1, total), jnp.asarray(table.T.copy()), norm)


def solution(mesh):
    return jax.shard_map(
        per_device,
        mesh=mesh,
        in_specs=(
            P(("member", "lat"), None, None),
            P(),
            P(),
            P("lat", None, None),
            P("lat", None, None, None),
        ),
        out_specs=P(("member", "lat"), None, None),
        check_vma=False,
    )
```

time: 104 us -> 75.2 us (0.72)
  blocking collectives: 35 us -> 0 us
  Pallas kernels: 0 us -> 26.7 us
  matrix products: 12.6 us -> 0 us
  other arithmetic: 9.31 us -> 1.02 us
  waiting for transfers between devices: 33 us -> 27.7 us
  starting transfers between devices: 8.95 us -> 12.1 us
  local copies, waits for them, and re-layouts: 4.87 us -> 6.85 us
    psum x1 -> x0, blocking collectives: 35 us -> none  [per_device(): total, squares = lax.psum((local_sum, local_sq), 'lat')]
    pallas_call x0 -> x4, Pallas kernels: none -> 26.7 us  [the longest x1 11.7 us: per_device(): pl.pallas_call(functools.partial(inverse_kernel, inv_root), grid=(lat_dev...]
    dot_general x4 -> x0, matrix products: 12.6 us -> none  [the longest x1 6.16 us: per_device(): jnp.einsum('akrc,rkn->anc', returned, inverse, preferred_element_type=jnp...]
    another operation x2 -> x0, other arithmetic: 5.69 us -> none
    all_to_all x2, waiting for transfers between devices: 33 us -> 27.7 us  [the longest x1 15.9 us: per_device(): lax.all_to_all(back.reshape(lat_count, rows, lanes), 'lat', split_axis=0,...]
    reduce_sum x1 -> x0, other arithmetic: 3.47 us -> none  [per_device(): local_sum = jnp.sum(values, axis=(0, 1))]
    all_to_all x2, starting transfers between devices: 8.95 us -> 12.1 us  [the longest x1 7.41 us: per_device(): lax.all_to_all(payload.reshape(lat_count, rows, lanes), 'lat', split_axis...]
    unnamed x8 -> x9, local copies, waits for them, and re-layouts: 0.02 us -> 2.33 us
  transfers between devices with their start and end apart: 2 -> 2, of which waited for: 2 -> 2; matrix products, arithmetic and copies ran while one was open for 4% -> 4% of each run, Pallas kernels for 0% -> 3%
where the time goes in v1:
time: 75.2 us; the launch traced here: 74.4 us
  waiting for transfers between devices  27.7 us (37%)
  Pallas kernels  26.7 us (36%)
  starting transfers between devices  12.1 us (16%)
  local copies, waits for them, and re-layouts  6.85 us (9%)
  other arithmetic  1.02 us (1%)
    all_to_all x1, waiting for transfers between devices, per_device(): lax.all_to_all(back.reshape(lat_count, rows, lanes), 'lat', split_axis=0,...  15.9 us
    all_to_all x1, waiting for transfers between devices, per_device(): lax.all_to_all(payload.reshape(lat_count, rows, lanes), 'lat', split_axis...  11.8 us
    pallas_call x1, Pallas kernels, per_device(): pl.pallas_call(functools.partial(inverse_kernel, inv_root), grid=(lat_dev...  11.7 us
    pallas_call x1, Pallas kernels, per_device(): pl.pallas_call(forward_kernel, grid=(steps,), in_specs=[pl.BlockSpec((1,...  7.52 us
    all_to_all x1, starting transfers between devices, per_device(): lax.all_to_all(payload.reshape(lat_count, rows, lanes), 'lat', split_axis...  7.41 us
    pallas_call x1, Pallas kernels, per_device(): pl.pallas_call(functools.partial(spectral_kernel, lat_count, float(lat_de...  5.39 us
    all_to_all x1, starting transfers between devices, per_device(): lax.all_to_all(back.reshape(lat_count, rows, lanes), 'lat', split_axis=0,...  4.67 us
    unnamed x9, local copies, waits for them, and re-layouts  2.33 us
  transfers between devices with their start and end apart: 2, of which 2 were waited for; matrix products, arithmetic and copies ran while one was open for 4% of the time, Pallas kernels for 3%

profile of v1, /device:TPU:0, one launch (start us, length us, event | category | flops | bytes accessed | tf_op | source)
XLA Modules:
  0.0 74.4 jit_solution(609518076159946777)
XLA Ops:
  0.0 0.0 copy-start.3
  0.0 0.8 %reshape.45 = s32[16,6]{1,0:T(8,128)S(1)} reshape(s32[96]{0:T(128)} %param.13) | data formatting | bytes 768 | tf_op jit(solution)/shard_map/reshape | solution.py:158
  0.8 0.1 copy.22
  0.9 0.1 add.30
  1.0 0.1 copy.21
  1.1 0.1 add_select_fusion
  1.2 0.1 copy.23
  1.3 0.8 %pad_add_fusion = s32[16,40]{1,0:T(8,128)S(1)} fusion(s32[16,4]{1,0:T(8,128)} %constant.10.clone, s32[16,36]{1,0:T(8,128)S(1)} %copy.23), kind=kLoop, calls=%fused_computation.2 | loop fusion | flops 640 | bytes 5120 | tf_op jit(solution)/shard_map/concatenate | solution.py:163
  2.1 0.9 %reshape.63.column = s32[640,1]{1,0:T(8,128)} reshape(s32[16,40]{1,0:T(8,128)S(1)} %pad_add_fusion) | data formatting | bytes 5120 | tf_op jit(solution)/shard_map/reshape | solution.py:185
  2.9 7.5 %forward.1 = bf16[640,512]{1,0:T(8,128)(2,1)} custom-call(bf16[6,1440,256]{2,1,0:T(8,128)(2,1)} %field.3, bf16[192,1440]{1,0:T(8,128)(2,1)} %constant.11.clone.table, f32[192,1]{1,0:T(8,128)} %constant.44.sums, s32[640,1]{1,0:T(8,128)} %reshape.63.column), custom_call_target="tpu_custom_call" | custom-call | tf_op jit(solution)/shard_map/forward/pallas_call | solution.py:166
  10.5 7.4 %all-to-all-start = ((bf16[16,40,512]{2,1,0:T(8,128)(2,1)}), bf16[16,40,512]{2,1,0:T(8,128)(2,1)S(1)}, u32[]{:S(2)}, u32[]{:S(2)}) async-start(bf16[16,40,512]{2,1,0:T(8,128)(2,1)} %bitcast.16), calls=%async_computation | async-start | bytes 1310720 | tf_op jit(solution)/shard_map/all_to_all | solution.py:186
  17.9 0.0 copy-done.3
  17.9 0.1 broadcast_compare_fusion.1
  18.0 0.0 copy-start.2
  18.0 1.4 %gather_fusion = f32[6,2]{1,0:T(8,128)S(1)} fusion(f32[2,96]{0,1:T(8,128)} %constant.37.clone, s32[1024]{0:T(1024)S(1)} %pad_clamp_fusion), kind=kCustom, calls=%fused_computation | custom fusion | bytes 120 | tf_op jit(solution)/shard_map/gather | solution.py:206
  19.4 0.1 select_bitcast_fusion
  19.4 0.1 copy.25
  19.5 0.1 broadcast_in_dim.49
  19.6 0.1 reshape.49
  19.7 0.1 copy.26
  19.8 0.1 broadcast_in_dim.50
  19.9 0.6 copy.27
  20.5 2.1 %spread.1.wide = bf16[576,640]{1,0:T(8,128)(2,1)} custom-call(bf16[6,96,96]{2,1,0:T(8,128)(2,1)} %legendre.1, s32[6,640]{1,0:T(8,128)} %constant.36.clone.place), custom_call_target="tpu_custom_call" | custom-call | flops 70778880 | tf_op jit(solution)/shard_map/spread/pallas_call | solution.py:193
  22.7 11.8 %all-to-all-done = bf16[16,40,512]{2,1,0:T(8,128)(2,1)S(1)} async-done(((bf16[16,40,512]{2,1,0:T(8,128)(2,1)}), bf16[16,40,512]{2,1,0:T(8,128)(2,1)S(1)}, u32[]{:S(2)}, u32[]{:S(2)}) %all-to-all-start) | async-done | bytes 655392 | tf_op jit(solution)/shard_map/all_to_all | solution.py:186
  34.5 0.0 copy-start.1
  34.5 0.0 copy-done.2
  34.5 0.8 %copy-done.1 = bf16[16,40,512]{2,1,0:T(8,128)(2,1)} copy-done((bf16[16,40,512]{2,1,0:T(8,128)(2,1)}, bf16[16,40,512]{2,1,0:T(8,128)(2,1)S(1)}, u32[]{:S(2)}) %copy-start.1) | copy-done | bytes 655384
  35.3 5.4 %spectral.1 = (bf16[640,512]{1,0:T(8,128)(2,1)}, f32[8,256]{1,0:T(8,128)}) custom-call(s32[6]{0:T(128)} %copy-done.2, bf16[640,512]{1,0:T(8,128)(2,1)} %bitcast.17, bf16[576,640]{1,0:T(8,128)(2,1)} %spread.1.wide, bf16[6,2,256,256]{3,2,1,0:T(8,128)(2,1)} %mixing.1, f32[1,256]{1,0:T(1,128)} %bitcast.21, f32[40,512]{1,0:T(8,128)} %bitcast.19), custom_call_target="tpu_custom_call" | custom-call | tf_op jit(solution)/shard_map/spectral/pallas_call | solution.py:210
  40.7 4.7 %all-to-all-start.1 = ((bf16[16,40,512]{2,1,0:T(8,128)(2,1)}), bf16[16,40,512]{2,1,0:T(8,128)(2,1)S(1)}, u32[]{:S(2)}, u32[]{:S(2)}) async-start(bf16[16,40,512]{2,1,0:T(8,128)(2,1)} %bitcast.18), calls=%async_computation.1 | async-start | bytes 1310720 | tf_op jit(solution)/shard_map/all_to_all | solution.py:227
  45.4 0.7 reshape.53.column
  46.0 15.9 %all-to-all-done.1 = bf16[16,40,512]{2,1,0:T(8,128)(2,1)S(1)} async-done(((bf16[16,40,512]{2,1,0:T(8,128)(2,1)}), bf16[16,40,512]{2,1,0:T(8,128)(2,1)S(1)}, u32[]{:S(2)}, u32[]{:S(2)}) %all-to-all-start.1) | async-done | bytes 655392 | tf_op jit(solution)/shard_map/all_to_all | solution.py:227
  61.9 0.0 copy-start
  62.0 0.8 %copy-done = bf16[16,40,512]{2,1,0:T(8,128)(2,1)} copy-done((bf16[16,40,512]{2,1,0:T(8,128)(2,1)}, bf16[16,40,512]{2,1,0:T(8,128)(2,1)S(1)}, u32[]{:S(2)}) %copy-start) | copy-done | bytes 655384
  62.8 11.7 %inverse.1 = bf16[6,1440,256]{2,1,0:T(8,128)(2,1)} custom-call(bf16[6,1440,256]{2,1,0:T(8,128)(2,1)} %field.3, bf16[640,512]{1,0:T(8,128)(2,1)} %bitcast.15, s32[1,640]{1,0:T(1,128)} %reshape.53.column, bf16[1440,192]{1,0:T(8,128)(2,1)} %constant.38.clone.table, f32[8,256]{1,0:T(8,128)} %get-tuple-element.8.norm), custom_call_target="tpu_custom_call" | custom-call | tf_op jit(solution)/shard_map/inverse/pallas_call | solution.py:232
  (10 shorter events, 0.1 us)
Async XLA Ops:
  0.0 17.9 %copy-start.3 = (s32[96]{0:T(128)S(1)}, s32[96]{0:T(128)}, u32[]{:S(2)}) copy-start(s32[96]{0:T(128)} %param.13) | copy-start | bytes 1156
  10.5 24.0 %all-to-all-start = ((bf16[16,40,512]{2,1,0:T(8,128)(2,1)}), bf16[16,40,512]{2,1,0:T(8,128)(2,1)S(1)}, u32[]{:S(2)}, u32[]{:S(2)}) async-start(bf16[16,40,512]{2,1,0:T(8,128)(2,1)} %bitcast.16), calls=%async_computation | async-start | bytes 1310720 | tf_op jit(solution)/shard_map/all_to_all | solution.py:186
  18.0 16.5 %copy-start.2 = (s32[6]{0:T(128)}, s32[6]{0:T(128)S(1)}, u32[]{:S(2)}) copy-start(s32[6]{0:T(128)S(1)} %get-tuple-element.10.mine) | copy-start | bytes 76
  34.5 0.8 %copy-start.1 = (bf16[16,40,512]{2,1,0:T(8,128)(2,1)}, bf16[16,40,512]{2,1,0:T(8,128)(2,1)S(1)}, u32[]{:S(2)}) copy-start(bf16[16,40,512]{2,1,0:T(8,128)(2,1)S(1)} %all-to-all-done) | copy-start | bytes 1966084
  40.7 21.3 %all-to-all-start.1 = ((bf16[16,40,512]{2,1,0:T(8,128)(2,1)}), bf16[16,40,512]{2,1,0:T(8,128)(2,1)S(1)}, u32[]{:S(2)}, u32[]{:S(2)}) async-start(bf16[16,40,512]{2,1,0:T(8,128)(2,1)} %bitcast.18), calls=%async_computation.1 | async-start | bytes 1310720 | tf_op jit(solution)/shard_map/all_to_all | solution.py:227
  61.9 0.8 %copy-start = (bf16[16,40,512]{2,1,0:T(8,128)(2,1)}, bf16[16,40,512]{2,1,0:T(8,128)(2,1)S(1)}, u32[]{:S(2)}) copy-start(bf16[16,40,512]{2,1,0:T(8,128)(2,1)S(1)} %all-to-all-done.1) | copy-start | bytes 1966084

commit v2 on v1

v2 whole, which is shorter than its diff:
```python
import functools
import math

import jax
import jax.numpy as jnp
import numpy as np
from jax import lax
from jax.experimental import pallas as pl
from jax.experimental.pallas import tpu as pltpu
from jax.sharding import PartitionSpec as P

F32 = jnp.float32
BF16 = jnp.bfloat16
PIECES = 3
EXTRA = 16


def dot(a, b, dims=((1,), (0,))):
    return lax.dot_general(a, b, (dims, ((), ())), preferred_element_type=F32)


def wave_tables(degs, width):
    turns = np.outer(np.arange(degs), np.arange(width)) % width
    phase = turns.astype(np.float64) * (2.0 * math.pi / width)
    table = np.concatenate([np.cos(phase), -np.sin(phase)]).astype(BF16)
    return table, table.astype(np.float64).sum(axis=1).astype(np.float32)


def slot_index(lookup, slot_wave, degs):
    depth = lookup.shape[1]
    slots = slot_wave.shape[1]
    lane = lax.broadcasted_iota(jnp.int32, (1, depth), 1)
    ends = jnp.where(lane == depth - 3, degs, jnp.where(lane == depth - 2, 1, -1))
    wave = jnp.concatenate(
        [jnp.where(slot_wave < degs, slot_wave, -16384), jnp.zeros((1, depth - slots), jnp.int32)],
        axis=1,
    )
    wave = jnp.broadcast_to(jnp.where(lane < slots, wave, ends), (128, depth))
    high = (wave >> 4).astype(F32).astype(BF16)
    low = (wave & 15).astype(F32).astype(BF16)
    nt = ((1,), (1,))
    return (dot(lookup, high, nt) * 16.0 + dot(lookup, low, nt)).astype(jnp.int32)


def forward_kernel(field, table, sums, waves, lookup, payload, packed, pick, shift, acc):
    step = pl.program_id(0)
    steps = pl.num_programs(0)
    rows, width = table.shape
    degs = rows // 2
    chans = field.shape[2]
    total, depth = pick.shape
    chunk = total // max(k for k in (1, 2, 4, 5) if total % (8 * k) == 0)
    opening = step == 0
    spec = dot(table[...], field[0])
    origin = jnp.where(opening, field[0, 0:16].astype(F32)[0:1], shift[1:2])
    total1 = jnp.where(opening, 0.0, acc[0])
    total2 = jnp.where(opening, 0.0, acc[1])
    part = width // max(k for k in range(1, 33) if width % (16 * k) == 0)
    for start in range(0, width, part):
        block = field[0, start : start + part]
        moved = block.astype(F32).reshape(part // 8, 8, chans) - origin
        total1 = total1 + jnp.sum(moved, axis=0)
        total2 = total2 + jnp.sum(moved * moved, axis=0)
    acc[0] = total1
    acc[1] = total2
    place = pl.ds(pl.multiple_of(jnp.minimum(step, total // chunk - 1) * chunk, chunk), chunk)
    index = slot_index(lookup[place], waves[...], degs)
    row = lax.broadcasted_iota(jnp.int32, (chunk, depth), 1)
    pick[place] = (row == index[:, 0:1]).astype(F32).astype(BF16)
    middle = jnp.where(opening, (spec[0:1] / width).astype(BF16).astype(F32), shift[0:1])
    shift[0:1] = middle
    shift[1:2] = origin
    centred = (spec - sums[...] * middle).astype(BF16)
    packed[pl.ds(step * degs, degs), :chans] = centred[:degs]
    packed[pl.ds(step * degs, degs), chans:] = centred[degs:]

    @pl.when(step == steps - 1)
    def _():
        count = float(width * (packed.shape[0] - EXTRA) // degs)
        delta = jnp.sum(acc[0], axis=0, keepdims=True) / count
        square = jnp.sum(acc[1], axis=0, keepdims=True)
        spread = jnp.maximum(square - count * delta * delta, 0.0)
        delta = (shift[1:2] - shift[0:1]) + delta
        lane = lax.broadcasted_iota(jnp.int32, (EXTRA, chans), 0)
        left = jnp.where(lane == 0, shift[0:1], 0.0)
        right = jnp.zeros((EXTRA, chans), F32)
        for piece in (1, 2):
            part = delta.astype(BF16).astype(F32)
            left = jnp.where(lane == piece, part, left)
            delta = delta - part
        for piece in range(PIECES):
            part = spread.astype(BF16).astype(F32)
            right = jnp.where(lane == piece, part, right)
            spread = spread - part
        packed[depth - EXTRA :, :chans] = left.astype(BF16)
        packed[depth - EXTRA :, chans:] = right.astype(BF16)
        payload[...] = dot(pick[...], packed[...]).astype(BF16)


def spread_kernel(legendre, place, out):
    slots, degs, nlat = legendre.shape
    total = out.shape[1]
    lat = lax.broadcasted_iota(jnp.int32, (nlat, total), 0)
    for j in range(slots):
        pick = (lat == place[j : j + 1]).astype(F32).astype(BF16)
        out[j * degs : (j + 1) * degs] = dot(legendre[j], pick).astype(BF16)


def unpack_kernel(degs, norm, waves, lookup, unpack):
    del norm
    total = unpack.shape[1]
    index = slot_index(lookup[...], waves[...], degs).T[0:1]
    for a in range(unpack.shape[0] // degs):
        row = lax.broadcasted_iota(jnp.int32, (degs, total), 0) + a * degs
        unpack[a * degs : (a + 1) * degs] = (row == index).astype(F32).astype(BF16)


def spectral_kernel(
    lat_count, count, inv_root, lat_scale, mine, arrived, wide, mixing, gain, sums, back, norm, mixed
):
    total, lanes = arrived.shape
    chans = lanes // 2
    rows = total // lat_count
    slots = mixing.shape[0]
    degs = wide.shape[0] // slots
    data = arrived[...]
    pick_row = lax.broadcasted_iota(jnp.int32, (PIECES * lat_count, total), 0)
    pick_col = lax.broadcasted_iota(jnp.int32, (PIECES * lat_count, total), 1)
    first = rows - 4
    want = (pick_row % lat_count) * rows + first + pick_row // lat_count
    stats = dot((pick_col == want).astype(F32).astype(BF16), data)
    stats = stats.reshape(PIECES, lat_count, lanes)
    shift = stats[0, :, :chans]
    delta = stats[1, :, :chans] + stats[2, :, :chans]
    spread = stats[0, :, chans:] + (stats[1, :, chans:] + stats[2, :, chans:])
    base = shift[0:1]
    drift = (shift - base) + delta
    drift_mean = jnp.sum(drift, axis=0, keepdims=True) / lat_count
    mean = base + drift_mean
    drift = drift - drift_mean
    var = jnp.sum(spread + count * drift * drift, axis=0, keepdims=True) / (count * lat_count)
    offs = (shift - base) - drift_mean
    scale = gain[...] / jnp.sqrt(var + 1e-05)
    norm[0:1] = mean
    norm[1:2] = scale
    scale2 = jnp.concatenate([scale, scale], axis=1) * inv_root
    offs2 = jnp.concatenate([offs, offs], axis=1)
    full = data.astype(F32).reshape(lat_count, rows, lanes)
    full = (full + offs2[:, None, :] * sums[...][None]) * scale2[None]
    full = full.reshape(total, lanes).astype(BF16)
    coefs = dot(wide[...], full)
    degree = lax.broadcasted_iota(jnp.int32, (degs, lanes), 0)
    for j in range(slots):
        wave = mine[j]
        coef = coefs[j * degs : (j + 1) * degs]
        coef = jnp.where(degree >= wave, coef, 0.0).astype(BF16)
        re, im = coef[:, :chans], coef[:, chans:]
        w0, w1 = mixing[j, 0], mixing[j, 1]
        weight = jnp.where(wave == 0, 1.0, 2.0).astype(F32)
        out_re = (dot(re, w0) - dot(im, w1)).astype(BF16).astype(F32) * weight
        out_im = (dot(re, w1) + dot(im, w0)).astype(BF16).astype(F32) * weight
        mixed[j * degs : (j + 1) * degs, :chans] = out_re.astype(BF16)
        mixed[j * degs : (j + 1) * degs, chans:] = out_im.astype(BF16)
    back[...] = (dot(wide[...], mixed[...], ((0,), (0,))) * (lat_scale * inv_root)).astype(BF16)


def inverse_kernel(field, returned, unpack, table, norm, result, coefs):
    lats, rows, chans = coefs.shape
    degs = rows // 2
    step, part = pl.program_id(0), pl.program_id(1)
    width = table.shape[0]

    @pl.when((step == 0) & (part == 0))
    def _():
        values = dot(unpack[...], returned[...]).astype(BF16)
        for a in range(lats):
            value = values[a * degs : (a + 1) * degs]
            coefs[a, :degs] = value[:, :chans]
            coefs[a, degs:] = value[:, chans:]

    span = result.shape[1]
    base = part * span
    mean, scale = norm[0:1], norm[1:2]
    waves = coefs[step]
    chunk = span // max(k for k in (1, 3) if span % (16 * k) == 0)
    for start in range(0, span, chunk):
        place = pl.ds(pl.multiple_of(base + start, 16), chunk)
        filtered = dot(table[place], waves)
        normed = (field[0, start : start + chunk].astype(F32) - mean) * scale
        result[0, start : start + chunk] = (normed + filtered).astype(BF16)


def per_device(field, gain, slot_wave, legendre, mixing):
    lat_count = lax.axis_size("lat")
    lat_dev, width, chans = field.shape
    slot_dev, degs, nlat = legendre.shape
    lanes = 2 * chans
    data_rows = lat_dev * slot_dev
    rows = -(-(data_rows + PIECES + 1) // 8) * 8
    total = lat_count * rows
    inv_root = 1.0 / math.sqrt(width)
    table, sums = wave_tables(degs, width)
    whole = pl.BlockSpec(memory_space=pltpu.VMEM)

    slots = lat_count * slot_dev
    deep = -(-(slots + 3) // 128) * 128
    lookup = np.zeros((lat_count, rows, deep), np.float32)
    for d in range(lat_count):
        for j in range(slot_dev):
            for a in range(lat_dev):
                lookup[d, j * lat_dev + a, d * slot_dev + j] = 1
                lookup[d, j * lat_dev + a, deep - 3] = a
    base = data_rows
    lookup[:, base : base + PIECES, deep - 3] = lat_dev
    lookup[:, base : base + PIECES, deep - 2] = np.arange(PIECES)
    lookup[:, base + PIECES :, deep - 1] = 1
    lookup = jnp.asarray(lookup.reshape(total, deep).astype(BF16))
    waves = slot_wave[None]

    steps = lat_dev
    depth = steps * degs + EXTRA
    limit = (16 if total <= 1024 else 60) * 2**20
    payload = pl.pallas_call(
        forward_kernel,
        grid=(steps,),
        in_specs=[
            pl.BlockSpec((1, width, chans), lambda i: (i, 0, 0)),
            pl.BlockSpec((2 * degs, width), lambda i: (0, 0)),
            pl.BlockSpec((2 * degs, 1), lambda i: (0, 0)),
            pl.BlockSpec((1, slots), lambda i: (0, 0)),
            pl.BlockSpec((total, deep), lambda i: (0, 0)),
        ],
        out_specs=whole,
        out_shape=jax.ShapeDtypeStruct((total, lanes), BF16),
        scratch_shapes=[
            pltpu.VMEM((depth, lanes), BF16),
            pltpu.VMEM((total, depth), BF16),
            pltpu.VMEM((8, chans), F32),
            pltpu.VMEM((2, 8, chans), F32),
        ],
        compiler_params=pltpu.CompilerParams(
            dimension_semantics=("arbitrary",),
            vmem_limit_bytes=max(limit, 56 * 2**20),
        ),
        name="forward",
    )(field, jnp.asarray(table), jnp.asarray(sums)[:, None], waves, lookup)
    arrived = lax.all_to_all(
        payload.reshape(lat_count, rows, lanes), "lat", split_axis=0, concat_axis=0, tiled=True
    ).reshape(total, lanes)

    place = np.full((slot_dev, lat_count, rows), -1, np.int32)
    for j in range(slot_dev):
        place[j, :, j * lat_dev : (j + 1) * lat_dev] = np.arange(nlat).reshape(lat_count, lat_dev)
    wide = pl.pallas_call(
        spread_kernel,
        in_specs=[whole] * 2,
        out_specs=whole,
        out_shape=jax.ShapeDtypeStruct((slot_dev * degs, total), BF16),
        cost_estimate=pl.CostEstimate(
            flops=2 * slot_dev * degs * nlat * total, bytes_accessed=0, transcendentals=0
        ),
        compiler_params=pltpu.CompilerParams(vmem_limit_bytes=limit),
        name="spread",
    )(legendre, jnp.asarray(place.reshape(slot_dev, total)))

    mine = lax.dynamic_slice_in_dim(slot_wave, lax.axis_index("lat") * slot_dev, slot_dev, 0)
    pair = jnp.asarray(np.stack([sums[:degs], sums[degs:]]))
    known = jnp.where(mine < degs, pair[:, jnp.minimum(mine, degs - 1)], 0.0)
    known = jnp.repeat(known, lat_dev, axis=1)
    known = jnp.pad(known, ((0, 0), (0, rows - data_rows)))
    known = jnp.broadcast_to(known.T[:, :, None], (rows, 2, chans)).reshape(rows, lanes)
    back, norm = pl.pallas_call(
        functools.partial(
            spectral_kernel,
            lat_count,
            float(lat_dev * width),
            inv_root,
            math.sqrt(nlat / degs),
        ),
        in_specs=[pl.BlockSpec(memory_space=pltpu.SMEM)] + [whole] * 5,
        out_specs=(whole, whole),
        out_shape=(
            jax.ShapeDtypeStruct((total, lanes), BF16),
            jax.ShapeDtypeStruct((8, chans), F32),
        ),
        scratch_shapes=[pltpu.VMEM((slot_dev * degs, lanes), BF16)],
        compiler_params=pltpu.CompilerParams(vmem_limit_bytes=limit),
        name="spectral",
    )(mine, arrived, wide, mixing, gain[None], known)
    unpack = pl.pallas_call(
        functools.partial(unpack_kernel, degs),
        in_specs=[whole] * 3,
        out_specs=whole,
        out_shape=jax.ShapeDtypeStruct((lat_dev * degs, total), BF16),
        cost_estimate=pl.CostEstimate(flops=10**9, bytes_accessed=0, transcendentals=0),
        compiler_params=pltpu.CompilerParams(vmem_limit_bytes=limit),
        name="unpack",
    )(norm, waves, lookup)
    returned = lax.all_to_all(
        back.reshape(lat_count, rows, lanes), "lat", split_axis=0, concat_axis=0, tiled=True
    ).reshape(total, lanes)

    parts = 1
    return pl.pallas_call(
        inverse_kernel,
        grid=(lat_dev, parts),
        in_specs=[pl.BlockSpec((1, width // parts, chans), lambda i, k: (i, k, 0))] + [whole] * 4,
        out_specs=pl.BlockSpec((1, width // parts, chans), lambda i, k: (i, k, 0)),
        out_shape=jax.ShapeDtypeStruct(field.shape, BF16),
        scratch_shapes=[pltpu.VMEM((lat_dev, 2 * degs, chans), BF16)],
        compiler_params=pltpu.CompilerParams(
            dimension_semantics=("arbitrary", "arbitrary"), vmem_limit_bytes=60 * 2**20
        ),
        name="inverse",
    )(field, returned, unpack, jnp.asarray(table.T.copy()), norm)


def solution(mesh):
    return jax.shard_map(
        per_device,
        mesh=mesh,
        in_specs=(
            P(("member", "lat"), None, None),
            P(),
            P(),
            P("lat", None, None),
            P("lat", None, None, None),
        ),
        out_specs=P(("member", "lat"), None, None),
        check_vma=False,
    )
```

time: 75.2 us -> 66.1 us (0.88)
  Pallas kernels: 26.7 us -> 19.2 us
  local copies, waits for them, and re-layouts: 6.85 us -> 4.39 us
  waiting for transfers between devices: 27.7 us -> 29.5 us
  other arithmetic: 1.02 us -> 0.17 us
    pallas_call x2 -> x3, Pallas kernels: 13.8 us -> 8.77 us  [the longest x1 8.03 us: per_device(): pl.pallas_call(inverse_kernel, grid=(lat_dev, parts), in_specs=[pl.BlockS...]
    pallas_call x1, Pallas kernels: 5.39 us -> 2.5 us  [per_device(): pl.pallas_call(functools.partial(spectral_kernel, lat_count, float(lat_de...]
    reshape x4 -> x0, local copies, waits for them, and re-layouts: 2.42 us -> none  [the longest x2 0.88 us: per_device(): waves = slot_wave.reshape(lat_count, slot_dev, 1)]
    all_to_all x1, waiting for transfers between devices: 11.8 us -> 14.2 us  [per_device(): lax.all_to_all(payload.reshape(lat_count, rows, lanes), 'lat', split_axis...]
    concatenate x1 -> x0, other arithmetic: 0.77 us -> none  [per_device(): column = jnp.concatenate([source, jnp.asarray(tail)], axis=1)]
    unnamed x9 -> x21, local copies, waits for them, and re-layouts: 2.33 us -> 2.58 us
  transfers between devices with their start and end apart: 2 -> 2, of which waited for: 2 -> 2; matrix products, arithmetic and copies ran while one was open for 4% -> 3% of each run, Pallas kernels for 3% -> 1%
where the time goes in v2:
time: 66.1 us; the launch traced here: 65.6 us
  waiting for transfers between devices  29.5 us (45%)
  Pallas kernels  19.2 us (29%)
  starting transfers between devices  12.2 us (18%)
  local copies, waits for them, and re-layouts  4.39 us (7%)
    all_to_all x1, waiting for transfers between devices, per_device(): lax.all_to_all(back.reshape(lat_count, rows, lanes), 'lat', split_axis=0,...  15.3 us
    all_to_all x1, waiting for transfers between devices, per_device(): lax.all_to_all(payload.reshape(lat_count, rows, lanes), 'lat', split_axis...  14.2 us
    pallas_call x1, Pallas kernels, per_device(): pl.pallas_call(inverse_kernel, grid=(lat_dev, parts), in_specs=[pl.BlockS...  8.03 us
    pallas_call x1, Pallas kernels, per_device(): pl.pallas_call(forward_kernel, grid=(steps,), in_specs=[pl.BlockSpec((1,...  7.92 us
    all_to_all x1, starting transfers between devices, per_device(): lax.all_to_all(payload.reshape(lat_count, rows, lanes), 'lat', split_axis...  7.55 us
    all_to_all x1, starting transfers between devices, per_device(): lax.all_to_all(back.reshape(lat_count, rows, lanes), 'lat', split_axis=0,...  4.68 us
    unnamed x21, local copies, waits for them, and re-layouts  2.58 us
    pallas_call x1, Pallas kernels, per_device(): pl.pallas_call(functools.partial(spectral_kernel, lat_count, float(lat_de...  2.5 us
  transfers between devices with their start and end apart: 2, of which 2 were waited for; matrix products, arithmetic and copies ran while one was open for 3% of the time, Pallas kernels for 1%

profile of v2, /device:TPU:0, one launch (start us, length us, event | category | flops | bytes accessed | tf_op | source)
XLA Modules:
  0.0 65.6 jit_solution(14721006121358583417)
XLA Ops:
  0.0 0.0 copy-start.5
  0.0 0.0 copy-start.7
  0.0 0.0 copy-start.4
  0.0 0.0 copy-start
  0.0 0.0 copy-start.8
  0.0 7.9 %forward.1 = bf16[640,512]{1,0:T(8,128)(2,1)} custom-call(bf16[6,1440,256]{2,1,0:T(8,128)(2,1)} %field.3, bf16[192,1440]{1,0:T(8,128)(2,1)} %constant.30.clone.table, f32[192,1]{1,0:T(8,128)} %constant.40.sums, s32[1,96]{1,0:T(1,128)} %bitcast.15, bf16[640,128]{1,0:T(8,128)(2,1)} %constant.11.clone.lookup), custom_call_target="tpu_custom_call" | custom-call | tf_op jit(solution)/shard_map/forward/pallas_call | solution.py:223
  7.9 0.0 copy-start.3
  7.9 7.6 %all-to-all-start = ((bf16[16,40,512]{2,1,0:T(8,128)(2,1)}), bf16[16,40,512]{2,1,0:T(8,128)(2,1)S(1)}, u32[]{:S(2)}, u32[]{:S(2)}) async-start(bf16[16,40,512]{2,1,0:T(8,128)(2,1)} %bitcast.19), calls=%async_computation | async-start | bytes 1310720 | tf_op jit(solution)/shard_map/all_to_all | solution.py:247
  15.5 0.0 copy-done.7
  15.5 0.1 broadcast_compare_fusion
  15.6 1.4 %gather_fusion = f32[6,2]{1,0:T(8,128)S(1)} fusion(f32[2,96]{0,1:T(8,128)} %constant.33.clone, s32[1024]{0:T(1024)S(1)} %pad_clamp_fusion), kind=kCustom, calls=%fused_computation | custom fusion | bytes 120 | tf_op jit(solution)/shard_map/gather | solution.py:268
  17.0 0.1 select_bitcast_fusion
  17.0 0.1 copy.14
  17.1 0.1 broadcast_in_dim.35
  17.2 0.1 reshape.21
  17.3 0.1 copy.15
  17.4 0.1 broadcast_in_dim.36
  17.5 0.0 copy-done.5
  17.5 0.0 copy-done.4
  17.5 0.3 spread.1.wide
  17.9 14.2 %all-to-all-done = bf16[16,40,512]{2,1,0:T(8,128)(2,1)S(1)} async-done(((bf16[16,40,512]{2,1,0:T(8,128)(2,1)}), bf16[16,40,512]{2,1,0:T(8,128)(2,1)S(1)}, u32[]{:S(2)}, u32[]{:S(2)}) %all-to-all-start) | async-done | bytes 655392 | tf_op jit(solution)/shard_map/all_to_all | solution.py:247
  32.1 0.0 copy-done
  32.1 0.0 copy-done.8
  32.1 2.5 %spectral.1 = (bf16[640,512]{1,0:T(8,128)(2,1)S(1)}, f32[8,256]{1,0:T(8,128)S(1)}) custom-call(s32[6]{0:T(128)S(1)} %get-tuple-element.10.mine, bf16[640,512]{1,0:T(8,128)(2,1)S(1)} %bitcast.12, bf16[576,640]{1,0:T(8,128)(2,1)S(1)} %spread.1.wide, bf16[6,2,256,256]{3,2,1,0:T(8,128)(2,1)S(1)} %copy-done, f32[1,256]{1,0:T(1,128)S(1)} %bitcast.17, ...), custom_call_target="tpu_custom_call" | custom-call | tf_op jit(solution)/shard_map/spectral/pallas_call | solution.py:272
  34.6 0.0 copy-start.2
  34.6 0.8 %copy-done.2 = bf16[640,512]{1,0:T(8,128)(2,1)} copy-done((bf16[640,512]{1,0:T(8,128)(2,1)}, bf16[640,512]{1,0:T(8,128)(2,1)S(1)}, u32[]{:S(2)}) %copy-start.2) | copy-done | bytes 655384
  35.4 0.0 copy-start.6
  35.4 4.7 %all-to-all-start.1 = ((bf16[16,40,512]{2,1,0:T(8,128)(2,1)}), bf16[16,40,512]{2,1,0:T(8,128)(2,1)S(1)}, u32[]{:S(2)}, u32[]{:S(2)}) async-start(bf16[16,40,512]{2,1,0:T(8,128)(2,1)} %bitcast.13), calls=%async_computation.1 | async-start | bytes 1310720 | tf_op jit(solution)/shard_map/all_to_all | solution.py:299
  40.1 0.0 copy-done.3
  40.1 0.4 unpack.1
  40.5 0.0 copy-start.1
  40.5 0.9 %copy-done.1 = bf16[576,640]{1,0:T(8,128)(2,1)} copy-done((bf16[576,640]{1,0:T(8,128)(2,1)}, bf16[576,640]{1,0:T(8,128)(2,1)S(1)}, u32[]{:S(2)}) %copy-start.1) | copy-done | bytes 737304
  41.4 15.3 %all-to-all-done.1 = bf16[16,40,512]{2,1,0:T(8,128)(2,1)S(1)} async-done(((bf16[16,40,512]{2,1,0:T(8,128)(2,1)}), bf16[16,40,512]{2,1,0:T(8,128)(2,1)S(1)}, u32[]{:S(2)}, u32[]{:S(2)}) %all-to-all-start.1) | async-done | bytes 655392 | tf_op jit(solution)/shard_map/all_to_all | solution.py:299
  56.7 0.0 copy-start.9
  56.7 0.0 copy-done.6
  56.7 0.8 %copy-done.9 = bf16[16,40,512]{2,1,0:T(8,128)(2,1)} copy-done((bf16[16,40,512]{2,1,0:T(8,128)(2,1)}, bf16[16,40,512]{2,1,0:T(8,128)(2,1)S(1)}, u32[]{:S(2)}) %copy-start.9) | copy-done | bytes 655384
  57.5 8.0 %inverse.1 = bf16[6,1440,256]{2,1,0:T(8,128)(2,1)} custom-call(bf16[6,1440,256]{2,1,0:T(8,128)(2,1)} %field.3, bf16[640,512]{1,0:T(8,128)(2,1)} %bitcast.18, bf16[576,640]{1,0:T(8,128)(2,1)} %copy-done.1, bf16[1440,192]{1,0:T(8,128)(2,1)} %constant.34.clone.table, f32[8,256]{1,0:T(8,128)} %copy-done.6), custom_call_target="tpu_custom_call" | custom-call | tf_op jit(solution)/shard_map/inverse/pallas_call | solution.py:304
  (4 shorter events, 0.0 us)
Async XLA Ops:
  0.0 17.5 %copy-start.5 = (s32[6,640]{1,0:T(8,128)S(1)}, s32[6,640]{1,0:T(8,128)}, u32[]{:S(2)}) copy-start(s32[6,640]{1,0:T(8,128)} %constant.32.clone.place) | copy-start | bytes 46084
  0.0 15.5 %copy-start.7 = (s32[96]{0:T(128)S(1)}, s32[96]{0:T(128)}, u32[]{:S(2)}) copy-start(s32[96]{0:T(128)} %param.13) | copy-start | bytes 1156
  0.0 17.5 %copy-start.4 = (bf16[6,96,96]{2,1,0:T(8,128)(2,1)S(1)}, bf16[6,96,96]{2,1,0:T(8,128)(2,1)}, u32[]{:S(2)}) copy-start(bf16[6,96,96]{2,1,0:T(8,128)(2,1)} %legendre.1) | copy-start | bytes 331780
  0.0 32.1 %copy-start = (bf16[6,2,256,256]{3,2,1,0:T(8,128)(2,1)S(1)}, bf16[6,2,256,256]{3,2,1,0:T(8,128)(2,1)}, u32[]{:S(2)}) copy-start(bf16[6,2,256,256]{3,2,1,0:T(8,128)(2,1)} %mixing.1) | copy-start | bytes 4718596
  0.0 32.1 %copy-start.8 = (f32[256]{0:T(256)S(1)}, f32[256]{0:T(256)}, u32[]{:S(2)}) copy-start(f32[256]{0:T(256)} %param.12) | copy-start | bytes 3076
  7.9 32.2 %copy-start.3 = (bf16[640,128]{1,0:T(8,128)(2,1)S(1)}, bf16[640,128]{1,0:T(8,128)(2,1)}, u32[]{:S(2)}) copy-start(bf16[640,128]{1,0:T(8,128)(2,1)} %constant.11.clone.lookup) | copy-start | bytes 491524
  7.9 24.1 %all-to-all-start = ((bf16[16,40,512]{2,1,0:T(8,128)(2,1)}), bf16[16,40,512]{2,1,0:T(8,128)(2,1)S(1)}, u32[]{:S(2)}, u32[]{:S(2)}) async-start(bf16[16,40,512]{2,1,0:T(8,128)(2,1)} %bitcast.19), calls=%async_computation | async-start | bytes 1310720 | tf_op jit(solution)/shard_map/all_to_all | solution.py:247
  34.6 0.8 %copy-start.2 = (bf16[640,512]{1,0:T(8,128)(2,1)}, bf16[640,512]{1,0:T(8,128)(2,1)S(1)}, u32[]{:S(2)}) copy-start(bf16[640,512]{1,0:T(8,128)(2,1)S(1)} %get-tuple-element.7) | copy-start | bytes 1966084
  35.4 21.3 %copy-start.6 = (f32[8,256]{1,0:T(8,128)}, f32[8,256]{1,0:T(8,128)S(1)}, u32[]{:S(2)}) copy-start(f32[8,256]{1,0:T(8,128)S(1)} %get-tuple-element.8.norm) | copy-start | bytes 24580
  35.4 21.3 %all-to-all-start.1 = ((bf16[16,40,512]{2,1,0:T(8,128)(2,1)}), bf16[16,40,512]{2,1,0:T(8,128)(2,1)S(1)}, u32[]{:S(2)}, u32[]{:S(2)}) async-start(bf16[16,40,512]{2,1,0:T(8,128)(2,1)} %bitcast.13), calls=%async_computation.1 | async-start | bytes 1310720 | tf_op jit(solution)/shard_map/all_to_all | solution.py:299
  40.5 0.9 %copy-start.1 = (bf16[576,640]{1,0:T(8,128)(2,1)}, bf16[576,640]{1,0:T(8,128)(2,1)S(1)}, u32[]{:S(2)}) copy-start(bf16[576,640]{1,0:T(8,128)(2,1)S(1)} %unpack.1) | copy-start | bytes 2211844
  56.7 0.9 %copy-start.9 = (bf16[16,40,512]{2,1,0:T(8,128)(2,1)}, bf16[16,40,512]{2,1,0:T(8,128)(2,1)S(1)}, u32[]{:S(2)}) copy-start(bf16[16,40,512]{2,1,0:T(8,128)(2,1)S(1)} %all-to-all-done.1) | copy-start | bytes 1966084
